TPU v7x, 256 devices: a whole 4x4x8 slice. The times are simulated.
256 devices in a mesh: shard: 64 (over z, y, core), col: 4 (over x).
Axes of the slice: x: 4, y: 4, z: 8, core: 2. Of those that a mesh axis runs over, the one named last changes fastest.
Arguments:
- values: float32 [32768, 512], P('shard', 'col'), may hold values from -6 to 6
- keep_mask: int32 [32768], P(('shard', 'col')), may hold values from 0 to 1, as said below
- row_counts: int32 [64], P('shard'), may hold values from 128 to 512
Outputs:
- packed: float32 [32768, 512], P('shard', 'col')
- span_stats: float32 [4, 64, 512], P(None, 'shard', 'col')
Inputs may be any that keep to these rules, and one draw needn't show every extreme that they name: `keep_mask`: mostly survivors, with delete-range gaps of 1 to 32 rows, denser in some regions.
All inputs are finite; a program needn't handle non-finite values.
Results may differ from a plain program's by a relative error of at most 0.00002.
Values sent between devices are 32-bit elements; how exact they have to be, the bound alone decides.
A program may use at most 128 MiB of HBM per device.

v0:
```python
import jax
import jax.numpy as jnp
from jax import lax
from jax.sharding import Mesh
from jax.sharding import PartitionSpec as P

SHARD = ("shard_0", "shard_1", "shard_2")
SHARD_COL = ("shard_0", "shard_1", "shard_2", "col")


def in_order(pieces, dim):
    lengths = list(pieces.shape[1:])
    lengths[dim] *= pieces.shape[0]
    return jnp.moveaxis(pieces, 0, dim).reshape(lengths)


def copy_for_each(value, axis):
    copies = jnp.broadcast_to(value, (lax.axis_size(axis), *value.shape))
    return lax.all_to_all(copies, axis, split_axis=0, concat_axis=0, tiled=True)


def gather_directly(value, axis, dim):
    return in_order(copy_for_each(value, axis), dim)


def whole_of(value, axes, dim):
    result = value
    for number in range(len(axes) - 1, -1, -1):
        result = lax.all_gather(result, axes[number], axis=dim, tiled=True)
    return result


def passed_along(value, axis, steps):
    count = lax.axis_size(axis)
    leading, last = (max(0, -steps), min(count, count - steps))
    return lax.ppermute(value, axis, [(source, source + steps) for source in range(leading, last)])


def on_device(values, keep_mask, row_counts):
    rows = values.shape[0]
    width = values.shape[1]
    shard_count = lax.axis_size(SHARD)
    shard_pos = lax.axis_index(SHARD)
    mask_full = gather_directly(keep_mask, "col", 0)
    local_index = jnp.arange(rows, dtype=jnp.int32)
    live = (mask_full == 1) & (local_index < row_counts[0])
    live_int = live.astype(jnp.int32)
    kept = jnp.sum(live_int)
    every = whole_of(kept[None], SHARD, 0)
    earlier = jnp.arange(shard_count, dtype=jnp.int32) < shard_pos
    offset = jnp.sum(jnp.where(earlier, every, 0))
    total = jnp.sum(every)
    start = shard_count * rows - total
    rank = jnp.cumsum(live_int) - live_int
    target = start + offset + rank
    cleaned = jnp.where(live[:, None], values, 0.0)
    base_owner = (start + offset) // rows
    window_slot = jnp.where(live, target - base_owner * rows, 2 * rows)
    window = jnp.zeros((2 * rows, width), jnp.float32).at[window_slot].set(cleaned, mode="drop")
    owner_code = jnp.where(kept > 0, base_owner + 1, 0)
    shard_bits = shard_count.bit_length() - 1
    for bit in range(shard_bits):
        remaining = owner_code - 1 - shard_pos
        moving = (owner_code > 0) & (remaining >> bit & 1 == 1)
        move_window = jnp.where(moving, window, 0.0)
        stay_window = jnp.where(moving, 0.0, window)
        move_code = jnp.where(moving, owner_code, 0)
        stay_code = jnp.where(moving, 0, owner_code)
        arrive_window, arrive_code = passed_along((move_window, move_code[None]), SHARD, 1 << bit)
        window = stay_window + arrive_window
        owner_code = jnp.maximum(stay_code, arrive_code[0])
    spilled = passed_along(window[rows:], SHARD, 1)
    packed = window[:rows] + spilled
    filled = jnp.clip((shard_pos + 1) * rows - start, 0, rows)
    row_live = (local_index >= rows - filled)[:, None]
    denom = jnp.maximum(filled.astype(jnp.float32), 1.0)
    mean = jnp.sum(packed, axis=0) / denom
    variance = jnp.sum(jnp.where(row_live, (packed - mean[None, :]) ** 2, 0.0), axis=0) / denom
    has_rows = filled > 0
    low = jnp.where(has_rows, jnp.min(jnp.where(row_live, packed, jnp.inf), axis=0), 0.0)
    high = jnp.where(has_rows, jnp.max(jnp.where(row_live, packed, -jnp.inf), axis=0), 0.0)
    span_stats = jnp.stack([mean, variance, low, high])[:, None, :]
    return (packed, span_stats)


def solution(mesh):
    finer = Mesh(
        mesh.devices.reshape(8, 4, 2, mesh.shape["col"]), ("shard_0", "shard_1", "shard_2", "col")
    )
    in_specs = (P(SHARD, "col"), P(SHARD_COL), P(SHARD))
    out_specs = (P(SHARD, "col"), P(None, SHARD, "col"))
    return jax.shard_map(
        on_device, mesh=finer, in_specs=in_specs, out_specs=out_specs, check_vma=False
    )
```

profile of v0, /device:TPU:168, one launch (start us, length us, event | category | flops | bytes accessed | tf_op | source)
XLA Modules:
  0.0 174.7 jit_solution(13053924160999751820)
XLA Ops:
  1.9 4.3 %all-to-all-start = ((s32[4,1,128]{2,1,0:T(1,128)}), s32[4,1,128]{2,1,0:T(1,128)S(1)}, u32[]{:S(2)}, u32[]{:S(2)}) async-start(s32[4,1,128]{2,1,0:T(1,128)} %broadcast_in_dim.88), calls=%async_computation | async-start | bytes 4096 | tf_op jit(solution)/shard_map/all_to_all | solution.py:19
  12.0 1.4 dynamic-update-slice
  13.5 1.8 %all-reduce = s32[2]{0:T(128)S(1)} all-reduce(s32[2]{0:T(128)S(1)} %dynamic-update-slice), channel_id=1, replica_groups=mesh['shard_0'=8,'shard_1'=4,'shard_2'=2,'col'=4] {'shard_2'}, use_global_device_ids=true, to_apply=%add | all-reduce | flops 2 | bytes 16
  15.5 8.2 %all-reduce.1 = s32[8]{0:T(128)S(1)} all-reduce(s32[8]{0:T(128)S(1)} %dynamic-update-slice.1), channel_id=1, replica_groups=mesh['shard_0'=8,'shard_1'=4,'shard_2'=2,'col'=4] {'shard_1'}, use_global_device_ids=true, to_apply=%add.1 | all-reduce | flops 8 | bytes 64
  23.8 10.4 %all-reduce.2 = s32[64]{0:T(128)S(1)} all-reduce(s32[64]{0:T(128)S(1)} %dynamic-update-slice.2), channel_id=1, replica_groups=mesh['shard_0'=8,'shard_1'=4,'shard_2'=2,'col'=4] {'shard_0'}, use_global_device_ids=true, to_apply=%add.2 | all-reduce | flops 64 | bytes 512
  37.5 2.4 %scatter_custom_fusion = f32[1024,128]{1,0:T(8,128)S(1)} fusion(s32[512]{0:T(512)S(1)} %bitcast.42, f32[512,128]{1,0:T(8,128)} %param.3, f32[]{:T(128)} %constant.66.clone.1, pred[512]{0:T(512)(128)(4,1)S(1)} %fusion.7), kind=kCustom, calls=%fused_computation.11 | custom fusion | flops 65536 | bytes 787968 | tf_op jit(solution)/shard_map/scatter | solution.py:59
  39.9 1.9 %collective-permute-start.5 = (f32[1024,128]{1,0:T(8,128)S(1)}, f32[1024,128]{1,0:T(8,128)S(1)}, u32[]{:S(2)}, u32[]{:S(2)}) collective-permute-start(f32[1024,128]{1,0:T(8,128)S(1)} %broadcast_select_fusion.5), channel_id=1, source_target_pairs={{0,4},{4,8},{8,12},{12,16},{16,20},{20,24},{24,28},{28,32},{32,36}... | collective-permute-start | bytes 1572872 | tf_op jit(solution)/shard_map/ppermute | solution.py:36
  41.8 2.7 %collective-permute-start = (s32[1]{0:T(128)}, s32[1]{0:T(128)}, u32[]{:S(2)}, u32[]{:S(2)}) collective-permute-start(s32[1]{0:T(128)} %bitcast.5), channel_id=1, source_target_pairs={{0,4},{4,8},{8,12},{12,16},{16,20},{20,24},{24,28},{28,32},{32,36}... | collective-permute-start | bytes 20 | tf_op jit(solution)/shard_map/ppermute | solution.py:36
  44.6 5.9 %collective-permute-done = s32[1]{0:T(128)} collective-permute-done((s32[1]{0:T(128)}, s32[1]{0:T(128)}, u32[]{:S(2)}, u32[]{:S(2)}) %collective-permute-start) | collective-permute-done | bytes 36 | tf_op jit(solution)/shard_map/ppermute | solution.py:36
  51.2 1.9 %collective-permute-start.6 = (f32[1024,128]{1,0:T(8,128)S(1)}, f32[1024,128]{1,0:T(8,128)S(1)}, u32[]{:S(2)}, u32[]{:S(2)}) collective-permute-start(f32[1024,128]{1,0:T(8,128)S(1)} %broadcast_select_fusion.4), channel_id=1, source_target_pairs={{0,8},{4,12},{8,16},{12,20},{16,24},{20,28},{24,32},{28,36},{32,40... | collective-permute-start | bytes 1572872 | tf_op jit(solution)/shard_map/ppermute | solution.py:36
  53.2 10.8 %collective-permute-start.1 = (s32[1]{0:T(128)}, s32[1]{0:T(128)}, u32[]{:S(2)}, u32[]{:S(2)}) collective-permute-start(s32[1]{0:T(128)} %bitcast.7), channel_id=1, source_target_pairs={{0,8},{4,12},{8,16},{12,20},{16,24},{20,28},{24,32},{28,36},{32,40... | collective-permute-start | bytes 20 | tf_op jit(solution)/shard_map/ppermute | solution.py:36
  65.8 3.7 %collective-permute-start.7 = (f32[1024,128]{1,0:T(8,128)S(1)}, f32[1024,128]{1,0:T(8,128)S(1)}, u32[]{:S(2)}, u32[]{:S(2)}) collective-permute-start(f32[1024,128]{1,0:T(8,128)S(1)} %get-tuple-element.19), channel_id=1, source_target_pairs={{0,16},{4,20},{8,24},{12,28},{16,32},{20,36},{24,40},{28,44},{32,4... | collective-permute-start | bytes 1572872 | tf_op jit(solution)/shard_map/ppermute | solution.py:36
  69.5 9.0 %collective-permute-start.2 = (s32[1]{0:T(128)}, s32[1]{0:T(128)}, u32[]{:S(2)}, u32[]{:S(2)}) collective-permute-start(s32[1]{0:T(128)} %bitcast.9), channel_id=1, source_target_pairs={{0,16},{4,20},{8,24},{12,28},{16,32},{20,36},{24,40},{28,44},{32,4... | collective-permute-start | bytes 20 | tf_op jit(solution)/shard_map/ppermute | solution.py:36
  78.5 5.1 %collective-permute-done.2 = s32[1]{0:T(128)} collective-permute-done((s32[1]{0:T(128)}, s32[1]{0:T(128)}, u32[]{:S(2)}, u32[]{:S(2)}) %collective-permute-start.2) | collective-permute-done | bytes 36 | tf_op jit(solution)/shard_map/ppermute | solution.py:36
  84.4 1.9 %collective-permute-start.8 = (f32[1024,128]{1,0:T(8,128)S(1)}, f32[1024,128]{1,0:T(8,128)S(1)}, u32[]{:S(2)}, u32[]{:S(2)}) collective-permute-start(f32[1024,128]{1,0:T(8,128)S(1)} %broadcast_select_fusion.2), channel_id=1, source_target_pairs={{0,32},{4,36},{8,40},{12,44},{16,48},{20,52},{24,56},{28,60},{32,6... | collective-permute-start | bytes 1572872 | tf_op jit(solution)/shard_map/ppermute | solution.py:36
  86.3 10.4 %collective-permute-start.3 = (s32[1]{0:T(128)}, s32[1]{0:T(128)}, u32[]{:S(2)}, u32[]{:S(2)}) collective-permute-start(s32[1]{0:T(128)} %bitcast.11), channel_id=1, source_target_pairs={{0,32},{4,36},{8,40},{12,44},{16,48},{20,52},{24,56},{28,60},{32,6... | collective-permute-start | bytes 20 | tf_op jit(solution)/shard_map/ppermute | solution.py:36
  96.7 2.2 %collective-permute-done.3 = s32[1]{0:T(128)} collective-permute-done((s32[1]{0:T(128)}, s32[1]{0:T(128)}, u32[]{:S(2)}, u32[]{:S(2)}) %collective-permute-start.3) | collective-permute-done | bytes 36 | tf_op jit(solution)/shard_map/ppermute | solution.py:36
  99.7 1.9 %collective-permute-start.9 = (f32[1024,128]{1,0:T(8,128)S(1)}, f32[1024,128]{1,0:T(8,128)S(1)}, u32[]{:S(2)}, u32[]{:S(2)}) collective-permute-start(f32[1024,128]{1,0:T(8,128)S(1)} %get-tuple-element.17), channel_id=1, source_target_pairs={{0,64},{4,68},{8,72},{12,76},{16,80},{20,84},{24,88},{28,92},{32,9... | collective-permute-start | bytes 1572872 | tf_op jit(solution)/shard_map/ppermute | solution.py:36
  101.7 20.8 %collective-permute-start.4 = (s32[1]{0:T(128)}, s32[1]{0:T(128)}, u32[]{:S(2)}, u32[]{:S(2)}) collective-permute-start(s32[1]{0:T(128)} %bitcast.13), channel_id=1, source_target_pairs={{0,64},{4,68},{8,72},{12,76},{16,80},{20,84},{24,88},{28,92},{32,9... | collective-permute-start | bytes 20 | tf_op jit(solution)/shard_map/ppermute | solution.py:36
  122.5 15.5 %collective-permute-done.4 = s32[1]{0:T(128)} collective-permute-done((s32[1]{0:T(128)}, s32[1]{0:T(128)}, u32[]{:S(2)}, u32[]{:S(2)}) %collective-permute-start.4) | collective-permute-done | bytes 36 | tf_op jit(solution)/shard_map/ppermute | solution.py:36
  138.8 1.3 collective-permute-start.10
  140.1 26.0 %collective-permute-done.10 = f32[1024,128]{1,0:T(8,128)S(1)} collective-permute-done((f32[1024,128]{1,0:T(8,128)S(1)}, f32[1024,128]{1,0:T(8,128)S(1)}, u32[]{:S(2)}, u32[]{:S(2)}) %collective-permute-start.10) | collective-permute-done | bytes 524320 | tf_op jit(solution)/shard_map/ppermute | solution.py:36
  166.2 1.9 %collective-permute-start.11 = (f32[512,128]{1,0:T(8,128)S(1)}, f32[512,128]{1,0:T(8,128)S(1)}, u32[]{:S(2)}, u32[]{:S(2)}) collective-permute-start(f32[512,128]{1,0:T(8,128)S(1)} %slice.18), channel_id=1, source_target_pairs={{0,4},{4,8},{8,12},{12,16},{16,20},{20,24},{24,28},{28,32},{32,36}... | collective-permute-start | bytes 786440 | tf_op jit(solution)/shard_map/ppermute | solution.py:36
  168.1 5.7 %collective-permute-done.11 = f32[512,128]{1,0:T(8,128)S(1)} collective-permute-done((f32[512,128]{1,0:T(8,128)S(1)}, f32[512,128]{1,0:T(8,128)S(1)}, u32[]{:S(2)}, u32[]{:S(2)}) %collective-permute-start.11) | collective-permute-done | bytes 262176 | tf_op jit(solution)/shard_map/ppermute | solution.py:36
  (50 shorter events, 9.3 us)
Async XLA Ops:
  1.9 9.5 %all-to-all-start = ((s32[4,1,128]{2,1,0:T(1,128)}), s32[4,1,128]{2,1,0:T(1,128)S(1)}, u32[]{:S(2)}, u32[]{:S(2)}) async-start(s32[4,1,128]{2,1,0:T(1,128)} %broadcast_in_dim.88), calls=%async_computation | async-start | bytes 4096 | tf_op jit(solution)/shard_map/all_to_all | solution.py:19
  6.8 0.7 copy-start.3
  7.5 0.7 copy-start.2
  8.2 0.7 copy-start.1
  39.9 11.3 %collective-permute-start.5 = (f32[1024,128]{1,0:T(8,128)S(1)}, f32[1024,128]{1,0:T(8,128)S(1)}, u32[]{:S(2)}, u32[]{:S(2)}) collective-permute-start(f32[1024,128]{1,0:T(8,128)S(1)} %broadcast_select_fusion.5), channel_id=1, source_target_pairs={{0,4},{4,8},{8,12},{12,16},{16,20},{20,24},{24,28},{28,32},{32,36}... | collective-permute-start | bytes 1572872 | tf_op jit(solution)/shard_map/ppermute | solution.py:36
  41.8 8.6 %collective-permute-start = (s32[1]{0:T(128)}, s32[1]{0:T(128)}, u32[]{:S(2)}, u32[]{:S(2)}) collective-permute-start(s32[1]{0:T(128)} %bitcast.5), channel_id=1, source_target_pairs={{0,4},{4,8},{8,12},{12,16},{16,20},{20,24},{24,28},{28,32},{32,36}... | collective-permute-start | bytes 20 | tf_op jit(solution)/shard_map/ppermute | solution.py:36
  51.2 14.4 %collective-permute-start.6 = (f32[1024,128]{1,0:T(8,128)S(1)}, f32[1024,128]{1,0:T(8,128)S(1)}, u32[]{:S(2)}, u32[]{:S(2)}) collective-permute-start(f32[1024,128]{1,0:T(8,128)S(1)} %broadcast_select_fusion.4), channel_id=1, source_target_pairs={{0,8},{4,12},{8,16},{12,20},{16,24},{20,28},{24,32},{28,36},{32,40... | collective-permute-start | bytes 1572872 | tf_op jit(solution)/shard_map/ppermute | solution.py:36
  53.2 11.8 %collective-permute-start.1 = (s32[1]{0:T(128)}, s32[1]{0:T(128)}, u32[]{:S(2)}, u32[]{:S(2)}) collective-permute-start(s32[1]{0:T(128)} %bitcast.7), channel_id=1, source_target_pairs={{0,8},{4,12},{8,16},{12,20},{16,24},{20,28},{24,32},{28,36},{32,40... | collective-permute-start | bytes 20 | tf_op jit(solution)/shard_map/ppermute | solution.py:36
  65.8 18.5 %collective-permute-start.7 = (f32[1024,128]{1,0:T(8,128)S(1)}, f32[1024,128]{1,0:T(8,128)S(1)}, u32[]{:S(2)}, u32[]{:S(2)}) collective-permute-start(f32[1024,128]{1,0:T(8,128)S(1)} %get-tuple-element.19), channel_id=1, source_target_pairs={{0,16},{4,20},{8,24},{12,28},{16,32},{20,36},{24,40},{28,44},{32,4... | collective-permute-start | bytes 1572872 | tf_op jit(solution)/shard_map/ppermute | solution.py:36
  69.5 14.1 %collective-permute-start.2 = (s32[1]{0:T(128)}, s32[1]{0:T(128)}, u32[]{:S(2)}, u32[]{:S(2)}) collective-permute-start(s32[1]{0:T(128)} %bitcast.9), channel_id=1, source_target_pairs={{0,16},{4,20},{8,24},{12,28},{16,32},{20,36},{24,40},{28,44},{32,4... | collective-permute-start | bytes 20 | tf_op jit(solution)/shard_map/ppermute | solution.py:36
  84.4 15.2 %collective-permute-start.8 = (f32[1024,128]{1,0:T(8,128)S(1)}, f32[1024,128]{1,0:T(8,128)S(1)}, u32[]{:S(2)}, u32[]{:S(2)}) collective-permute-start(f32[1024,128]{1,0:T(8,128)S(1)} %broadcast_select_fusion.2), channel_id=1, source_target_pairs={{0,32},{4,36},{8,40},{12,44},{16,48},{20,52},{24,56},{28,60},{32,6... | collective-permute-start | bytes 1572872 | tf_op jit(solution)/shard_map/ppermute | solution.py:36
  86.3 12.6 %collective-permute-start.3 = (s32[1]{0:T(128)}, s32[1]{0:T(128)}, u32[]{:S(2)}, u32[]{:S(2)}) collective-permute-start(s32[1]{0:T(128)} %bitcast.11), channel_id=1, source_target_pairs={{0,32},{4,36},{8,40},{12,44},{16,48},{20,52},{24,56},{28,60},{32,6... | collective-permute-start | bytes 20 | tf_op jit(solution)/shard_map/ppermute | solution.py:36
  99.7 39.0 %collective-permute-start.9 = (f32[1024,128]{1,0:T(8,128)S(1)}, f32[1024,128]{1,0:T(8,128)S(1)}, u32[]{:S(2)}, u32[]{:S(2)}) collective-permute-start(f32[1024,128]{1,0:T(8,128)S(1)} %get-tuple-element.17), channel_id=1, source_target_pairs={{0,64},{4,68},{8,72},{12,76},{16,80},{20,84},{24,88},{28,92},{32,9... | collective-permute-start | bytes 1572872 | tf_op jit(solution)/shard_map/ppermute | solution.py:36
  101.7 36.3 %collective-permute-start.4 = (s32[1]{0:T(128)}, s32[1]{0:T(128)}, u32[]{:S(2)}, u32[]{:S(2)}) collective-permute-start(s32[1]{0:T(128)} %bitcast.13), channel_id=1, source_target_pairs={{0,64},{4,68},{8,72},{12,76},{16,80},{20,84},{24,88},{28,92},{32,9... | collective-permute-start | bytes 20 | tf_op jit(solution)/shard_map/ppermute | solution.py:36
  138.8 27.3 %collective-permute-start.10 = (f32[1024,128]{1,0:T(8,128)S(1)}, f32[1024,128]{1,0:T(8,128)S(1)}, u32[]{:S(2)}, u32[]{:S(2)}) collective-permute-start(f32[1024,128]{1,0:T(8,128)S(1)} %broadcast_select_fusion), channel_id=1, source_target_pairs={{0,128},{4,132},{8,136},{12,140},{16,144},{20,148},{24,152},{28,15... | collective-permute-start | bytes 1572872 | tf_op jit(solution)/shard_map/ppermute | solution.py:36
  166.2 7.7 %collective-permute-start.11 = (f32[512,128]{1,0:T(8,128)S(1)}, f32[512,128]{1,0:T(8,128)S(1)}, u32[]{:S(2)}, u32[]{:S(2)}) collective-permute-start(f32[512,128]{1,0:T(8,128)S(1)} %slice.18), channel_id=1, source_target_pairs={{0,4},{4,8},{8,12},{12,16},{16,20},{20,24},{24,28},{28,32},{32,36}... | collective-permute-start | bytes 786440 | tf_op jit(solution)/shard_map/ppermute | solution.py:36
  173.9 0.8 copy-start
where the time goes:
time: 175 us
  starting transfers between devices  72.6 us (41%)
  waiting for transfers between devices  62.1 us (35%)
  blocking collectives  20.3 us (12%)
  between operations  8.23 us (5%)
  local copies, waits for them, and re-layouts  5.9 us (3%)
  other arithmetic  5.52 us (3%)
    ppermute x12, starting transfers between devices, passed_along(): lax.ppermute(value, axis, [(source, source + steps) for source in range(l...  68.3 us
    ppermute x12, waiting for transfers between devices, passed_along(): lax.ppermute(value, axis, [(source, source + steps) for source in range(l...  61.4 us
    unnamed x3, blocking collectives  20.3 us
    unnamed x17, local copies, waits for them, and re-layouts  4.45 us
    all_to_all x1, starting transfers between devices, copy_for_each(): return lax.all_to_all(copies, axis, split_axis=0, concat_axis=0, tiled=True)  4.29 us
  transfers between devices with their start and end apart: 13, of which 8 were waited for; matrix products, arithmetic and copies ran while one was open for 1% of the time, Pallas kernels for 0%

commit v1 on v0

v1 whole, which is shorter than its diff:
```python
import jax
import jax.numpy as jnp
from jax import lax
from jax.sharding import PartitionSpec as P


def gather_directly(value, axis):
    copies = jnp.broadcast_to(value, (lax.axis_size(axis), *value.shape))
    return lax.all_to_all(copies, axis, split_axis=0, concat_axis=0, tiled=True)


def on_device(values, keep_mask, row_counts):
    rows, width = values.shape
    shards = lax.axis_size("shard")
    tile = rows // shards
    me = lax.axis_index("shard")
    mask = gather_directly(keep_mask, "col").reshape(rows)
    local = jnp.arange(rows, dtype=jnp.int32)
    live = (mask == 1) & (local < row_counts[0])
    live_int = live.astype(jnp.int32)
    kept = jnp.sum(live_int)
    every = gather_directly(kept[None], "shard").reshape(shards)
    last = shards * rows - (jnp.sum(every) - jnp.cumsum(every))
    first = last - every
    rank = jnp.cumsum(live_int) - live_int
    place = jnp.where(live, (first[me] + rank) % rows, rows)
    pick = (local[:, None] == place[None, :]).astype(jnp.float32)
    block = jnp.dot(pick, values, precision=lax.Precision.HIGHEST)
    tiles = lax.all_to_all(block.reshape(shards, tile, width), "shard", 0, 0)
    sub = local % tile
    target = local // tile * rows + me * tile + sub
    fits = (first[local // tile][None, :] <= target[:, None]) & (target[:, None] < last[local // tile][None, :])
    mix = (fits & (sub[:, None] == sub[None, :])).astype(jnp.float32)
    mixed = jnp.dot(mix, tiles.reshape(rows, width), precision=lax.Precision.HIGHEST)
    packed = lax.all_to_all(mixed.reshape(shards, tile, width), "shard", 0, 0).reshape(rows, width)
    start = first[0]
    filled = jnp.clip((me + 1) * rows - start, 0, rows)
    row_live = (local >= rows - filled)[:, None]
    denom = jnp.maximum(filled.astype(jnp.float32), 1.0)
    mean = jnp.sum(packed, axis=0) / denom
    variance = jnp.sum(jnp.where(row_live, (packed - mean[None, :]) ** 2, 0.0), axis=0) / denom
    has_rows = filled > 0
    low = jnp.where(has_rows, jnp.min(jnp.where(row_live, packed, jnp.inf), axis=0), 0.0)
    high = jnp.where(has_rows, jnp.max(jnp.where(row_live, packed, -jnp.inf), axis=0), 0.0)
    span_stats = jnp.stack([mean, variance, low, high])[:, None, :]
    return (packed, span_stats)


def solution(mesh):
    in_specs = (P("shard", "col"), P(("shard", "col")), P("shard"))
    out_specs = (P("shard", "col"), P(None, "shard", "col"))
    return jax.shard_map(on_device, mesh=mesh, in_specs=in_specs, out_specs=out_specs, check_vma=False)
```

time: 175 us -> 159 us (0.909)
  the two profiles are of different devices: /device:TPU:168 before, /device:TPU:1 now
where the time goes in v1:
time: 159 us; the launch traced here: 157 us
  other arithmetic  87.1 us (55%)
  starting transfers between devices  33.7 us (21%)
  waiting for transfers between devices  22.5 us (14%)
  local copies, waits for them, and re-layouts  8.9 us (6%)
  matrix products  2.77 us (2%)
  between operations  2.16 us (1%)
    gather x59, other arithmetic, on_device(): first[local // tile][None, :] <= target[:, None]  41.9 us
    gather x2, other arithmetic, on_device(): last[local // tile][None, :]  40 us
    all_to_all x2, starting transfers between devices, gather_directly(): return lax.all_to_all(copies, axis, split_axis=0, concat_axis=0, tiled=True)  18.6 us
    all_to_all x1, waiting for transfers between devices, on_device(): lax.all_to_all(mixed.reshape(shards, tile, width), 'shard', 0, 0)  12.4 us
    all_to_all x1, starting transfers between devices, on_device(): lax.all_to_all(mixed.reshape(shards, tile, width), 'shard', 0, 0)  10.4 us
    all_to_all x2, waiting for transfers between devices, gather_directly(): return lax.all_to_all(copies, axis, split_axis=0, concat_axis=0, tiled=True)  10.2 us
    all_to_all x1, starting transfers between devices, on_device(): tiles = lax.all_to_all(block.reshape(shards, tile, width), 'shard', 0, 0)  4.73 us
  transfers between devices with their start and end apart: 4, of which 3 were waited for; matrix products, arithmetic and copies ran while one was open for 52% of the time, Pallas kernels for 0%

profile of v1, /device:TPU:1, one launch (start us, length us, event | category | flops | bytes accessed | tf_op | source)
XLA Modules:
  0.0 157.2 jit_solution(16983460072270758185)
XLA Ops:
  0.6 1.3 broadcast_in_dim.53
  1.9 4.8 %all-to-all-start = ((s32[4,1,128]{2,1,0:T(1,128)}), s32[4,1,128]{2,1,0:T(1,128)S(1)}, u32[]{:S(2)}, u32[]{:S(2)}) async-start(s32[4,1,128]{2,1,0:T(1,128)} %broadcast_in_dim.53), calls=%async_computation | async-start | bytes 4096 | tf_op jit(solution)/shard_map/all_to_all | solution.py:9
  9.4 1.4 all-to-all-done
  11.5 1.3 broadcast_in_dim.54
  12.7 13.8 %all-to-all-start.1 = ((s32[64,1,1]{2,1,0:T(1,128)}), s32[64,1,1]{2,1,0:T(1,128)S(1)}, u32[]{:S(2)}, u32[]{:S(2)}) async-start(s32[64,1,1]{2,1,0:T(1,128)} %broadcast_in_dim.54), calls=%async_computation.1 | async-start | bytes 65536 | tf_op jit(solution)/shard_map/all_to_all | solution.py:9
  27.0 8.8 %all-to-all-done.1 = s32[64,1,1]{2,1,0:T(1,128)S(1)} async-done(((s32[64,1,1]{2,1,0:T(1,128)}), s32[64,1,1]{2,1,0:T(1,128)S(1)}, u32[]{:S(2)}, u32[]{:S(2)}) %all-to-all-start.1) | async-done | bytes 288 | tf_op jit(solution)/shard_map/all_to_all | solution.py:9
  35.9 1.8 %fusion.34 = (s32[64]{0:T(128)S(1)}, s32[]{:T(128)}) fusion(s32[64,1,1]{2,1,0:T(1,128)S(1)} %all-to-all-done.1), kind=kLoop, calls=%fused_computation.135 | loop fusion | flops 63 | bytes 516 | tf_op jit(solution)/shard_map/all_to_all | solution.py:9
  37.7 0.7 fusion.35
  38.5 0.7 fusion.44
  39.2 0.7 fusion.45
  39.9 0.7 fusion.43
  42.5 0.7 fusion.40
  43.2 0.7 fusion.42
  43.9 0.7 fusion.23
  44.7 1.3 convolution_bitcast_fusion
  46.0 4.7 %all-to-all-start.2 = ((f32[64,8,128]{2,1,0:T(8,128)}), f32[64,8,128]{2,1,0:T(8,128)S(1)}, u32[]{:S(2)}, u32[]{:S(2)}) async-start(f32[64,8,128]{2,1,0:T(8,128)} %convolution_bitcast_fusion), calls=%async_computation.2 | async-start | bytes 524288 | tf_op jit(solution)/shard_map/all_to_all | solution.py:29
  50.7 4.4 %compare_select_fusion.1 = s32[512,1]{0,1:T(1,128)S(1)} fusion(s32[]{:T(128)} %bitcast.59, s32[]{:T(128)} %bitcast.60, s32[]{:T(128)} %bitcast.61, s32[]{:T(128)} %bitcast.62, s32[]{:T(128)} %bitcast.63, s32[]{:T(128)} %bitcast.65, s32[]{:T(128)} %bitcast.64), kind=kLoop, calls=%fused_computation.91 | loop fusion | flops 11776 | bytes 2076 | tf_op jit(solution)/shard_map/gather | solution.py:32
  55.2 4.5 %compare_select_fusion.2 = s32[512,1]{0,1:T(1,128)S(1)} fusion(s32[]{:T(128)} %bitcast.124, s32[]{:T(128)} %bitcast.125, s32[]{:T(128)} %bitcast.126, s32[]{:T(128)} %bitcast.127, s32[]{:T(128)} %bitcast.128, s32[]{:T(128)} %bitcast.130, s32[]{:T(128)} %bitcast.129), kind=kLoop, calls=%fused_computation.92 | loop fusion | flops 11776 | bytes 2076 | tf_op jit(solution)/shard_map/gather | solution.py:32
  59.6 35.5 %select_select_fusion.1 = s32[512]{0:T(512)S(1)} fusion(pred[512]{0:T(512)(128)(4,1)S(1)} %compare_reduce_fusion, pred[512]{0:T(512)(128)(4,1)S(1)} %compare_reduce_fusion.1, pred[512]{0:T(512)(128)(4,1)S(1)} %compare_reduce_fusion.2, pred[512]{0:T(512)(128)(4,1)S(1)} %compare_reduce_fusion.3, pred[512]{0:T(512)(128)(4,1)S(1)} %compare_reduce_fusion.4, ...), kind=kLoop, calls=%fused_computation.116 | loop fusion | flops 29184 | bytes 33508 | tf_op jit(solution)/shard_map/gather | solution.py:32
  95.2 35.5 %select_select_fusion = s32[512]{0:T(512)S(1)} fusion(pred[512]{0:T(512)(128)(4,1)S(1)} %compare_reduce_fusion, pred[512]{0:T(512)(128)(4,1)S(1)} %compare_reduce_fusion.1, pred[512]{0:T(512)(128)(4,1)S(1)} %compare_reduce_fusion.2, pred[512]{0:T(512)(128)(4,1)S(1)} %compare_reduce_fusion.3, pred[512]{0:T(512)(128)(4,1)S(1)} %compare_reduce_fusion.4, ...), kind=kLoop, calls=%fused_computation.115 | loop fusion | flops 29184 | bytes 33508 | tf_op jit(solution)/shard_map/gather | solution.py:32
  130.7 1.5 fusion
  132.2 10.4 %all-to-all-start.3 = ((f32[64,8,128]{2,1,0:T(8,128)}), f32[64,8,128]{2,1,0:T(8,128)S(1)}, u32[]{:S(2)}, u32[]{:S(2)}) async-start(f32[64,8,128]{2,1,0:T(8,128)} %fusion), calls=%async_computation.3 | async-start | bytes 524288 | tf_op jit(solution)/shard_map/all_to_all | solution.py:35
  143.3 12.4 %all-to-all-done.3 = f32[64,8,128]{2,1,0:T(8,128)S(1)} async-done(((f32[64,8,128]{2,1,0:T(8,128)}), f32[64,8,128]{2,1,0:T(8,128)S(1)}, u32[]{:S(2)}, u32[]{:S(2)}) %all-to-all-start.3) | async-done | bytes 262176 | tf_op jit(solution)/shard_map/all_to_all | solution.py:35
  156.5 0.7 copy.18
  (82 shorter events, 6.1 us)
Async XLA Ops:
  0.6 44.0 %copy-start = (f32[512,128]{1,0:T(8,128)S(1)}, f32[512,128]{1,0:T(8,128)}, u32[]{:S(2)}) copy-start(f32[512,128]{1,0:T(8,128)} %param.3) | copy-start | bytes 786436
  1.9 8.9 %all-to-all-start = ((s32[4,1,128]{2,1,0:T(1,128)}), s32[4,1,128]{2,1,0:T(1,128)S(1)}, u32[]{:S(2)}, u32[]{:S(2)}) async-start(s32[4,1,128]{2,1,0:T(1,128)} %broadcast_in_dim.53), calls=%async_computation | async-start | bytes 4096 | tf_op jit(solution)/shard_map/all_to_all | solution.py:9
  12.7 23.1 %all-to-all-start.1 = ((s32[64,1,1]{2,1,0:T(1,128)}), s32[64,1,1]{2,1,0:T(1,128)S(1)}, u32[]{:S(2)}, u32[]{:S(2)}) async-start(s32[64,1,1]{2,1,0:T(1,128)} %broadcast_in_dim.54), calls=%async_computation.1 | async-start | bytes 65536 | tf_op jit(solution)/shard_map/all_to_all | solution.py:9
  46.0 84.7 %all-to-all-start.2 = ((f32[64,8,128]{2,1,0:T(8,128)}), f32[64,8,128]{2,1,0:T(8,128)S(1)}, u32[]{:S(2)}, u32[]{:S(2)}) async-start(f32[64,8,128]{2,1,0:T(8,128)} %convolution_bitcast_fusion), calls=%async_computation.2 | async-start | bytes 524288 | tf_op jit(solution)/shard_map/all_to_all | solution.py:29
  132.2 23.5 %all-to-all-start.3 = ((f32[64,8,128]{2,1,0:T(8,128)}), f32[64,8,128]{2,1,0:T(8,128)S(1)}, u32[]{:S(2)}, u32[]{:S(2)}) async-start(f32[64,8,128]{2,1,0:T(8,128)} %fusion), calls=%async_computation.3 | async-start | bytes 524288 | tf_op jit(solution)/shard_map/all_to_all | solution.py:35

commit v2 on v1

v2 whole, which is shorter than its diff:
```python
import functools

import jax
import jax.numpy as jnp
from jax import lax
from jax.experimental import pallas as pl
from jax.experimental.pallas import tpu as pltpu
from jax.sharding import PartitionSpec as P

MESH = pl.DeviceIdType.MESH
CHUNKS = 2
SIZES = (8, 4, 2)


def hops(step):
    return sum(min(d, n - d) for d, n in zip(step[:2], SIZES[:2]))


STEPS = sorted(
    [(z, y, c) for z in range(8) for y in range(4) for c in range(2)][1:],
    key=lambda step: (-hops(step), step),
)


def iota(shape, dim):
    return lax.broadcasted_iota(jnp.int32, shape, dim)


def pieces(x):
    high = x.astype(jnp.bfloat16)
    rest = x - high.astype(jnp.float32)
    mid = rest.astype(jnp.bfloat16)
    low = (rest - mid.astype(jnp.float32)).astype(jnp.bfloat16)
    return jnp.concatenate([high, mid, low], axis=1)


def select(choice, parts):
    width = parts.shape[1] // 3
    out = jnp.dot(choice, parts, preferred_element_type=jnp.float32)
    return (out[:, :width] + out[:, width : 2 * width]) + out[:, 2 * width :]


def kernel(
    values_ref,
    mask_ref,
    counts_ref,
    packed_ref,
    stats_ref,
    values_buf,
    mask_own,
    mask_buf,
    counts_buf,
    kept_own,
    kept_buf,
    send_one,
    recv_one,
    send_two,
    recv_two,
    local_sem,
    mask_sem,
    kept_sem,
    one_sem,
    two_sem,
):
    rows, width = values_buf.shape
    shards = kept_buf.shape[0]
    unit = send_one.shape[2]
    span = shards * unit
    tile = rows // shards
    me = lax.axis_index("shard")
    col = lax.axis_index("col")

    load_mask = pltpu.make_async_copy(mask_ref, mask_own, local_sem.at[0])
    load_counts = pltpu.make_async_copy(counts_ref, counts_buf, local_sem.at[1])
    load_values = pltpu.make_async_copy(values_ref, values_buf, local_sem.at[2])
    load_mask.start()
    load_counts.start()
    load_values.start()

    z, y, c = me // 8, lax.rem(me // 2, 4), lax.rem(me, 2)
    peers = [
        lax.rem(z + dz, 8) * 8 + lax.rem(y + dy, 4) * 2 + lax.rem(c + dc, 2)
        for dz, dy, dc in STEPS
    ]
    cols = [lax.rem(col + d, 4) for d in (2, 1, 3)]

    barrier = pltpu.get_barrier_semaphore()
    for peer in peers:
        pl.semaphore_signal(barrier, inc=1, device_id={"shard": peer}, device_id_type=MESH)
    for peer in cols:
        pl.semaphore_signal(barrier, inc=1, device_id={"col": peer}, device_id_type=MESH)
    load_mask.wait()
    load_counts.wait()
    pl.semaphore_wait(barrier, len(peers) + len(cols))

    for peer in cols:
        pltpu.make_async_remote_copy(
            mask_own, mask_buf.at[col], mask_sem.at[0], mask_sem.at[1],
            device_id={"col": peer}, device_id_type=MESH,
        ).start()
    mask_buf[col] = mask_own[...]
    load_values.wait()
    parts = pieces(values_buf[...])
    three = mask_buf.at[pl.ds(0, len(cols))]
    pltpu.make_async_copy(three, three, mask_sem.at[1]).wait()

    groups = mask_buf.shape[0]
    mask = jnp.concatenate([mask_buf[g] for g in range(groups)], axis=0)
    row = iota((groups, width), 0) * width + iota((groups, width), 1)
    live = (mask == 1) & (row < counts_buf[0])
    live_part = jnp.where(live, 1.0, 0.0).astype(jnp.bfloat16)
    ahead = (iota((width, width), 0) < iota((width, width), 1)).astype(jnp.float32).astype(jnp.bfloat16)
    inside = jnp.dot(live_part, ahead, preferred_element_type=jnp.float32)
    ones = jnp.ones((width, width), jnp.bfloat16)
    whole = jnp.dot(live_part, ones, preferred_element_type=jnp.float32)
    kept = jnp.sum(whole, axis=0, keepdims=True)
    kept_own[...] = kept.astype(jnp.int32)
    for peer in peers:
        pltpu.make_async_remote_copy(
            kept_own, kept_buf.at[me], kept_sem.at[0], kept_sem.at[1],
            device_id={"shard": peer}, device_id_type=MESH,
        ).start()
    kept_buf[me] = kept_own[...]
    base = [jnp.zeros((1, width), jnp.float32)]
    for g in range(groups - 1):
        base.append(base[-1] + whole[g : g + 1])
    rank = (inside + jnp.concatenate(base, axis=0)).astype(jnp.int32)
    most = kept_buf.at[pl.ds(0, len(peers))]
    pltpu.make_async_copy(most, most, kept_sem.at[1]).wait()

    every = jnp.concatenate([kept_buf[i] for i in range(shards)], axis=0)
    shard = iota((shards, width), 0)
    mine = shards * rows - jnp.sum(jnp.where(shard >= me, every, 0), axis=0, keepdims=True)
    start = shards * rows - jnp.sum(every, axis=0, keepdims=True)
    target = mine + rank
    place = jnp.where(live, target - target // rows * rows, rows)

    index = iota((span, 1), 0)
    for h in range(CHUNKS):
        slot = index // unit * tile + unit * h + lax.rem(index, unit)
        choice = jnp.concatenate(
            [(slot == place[g : g + 1]).astype(jnp.float32).astype(jnp.bfloat16) for g in range(groups)], axis=1
        )
        send_one[h] = select(choice, parts).reshape(shards, unit, width)
        for peer in peers:
            pltpu.make_async_remote_copy(
                send_one.at[h, peer], recv_one.at[h, me], one_sem.at[0, h], one_sem.at[1, h],
                device_id={"shard": peer}, device_id_type=MESH,
            ).start()
        recv_one[h, me] = send_one[h, me]

    wide = jnp.concatenate([every] * max(1, span // width), axis=1)[:, :span]
    lane = iota((shards, span), 1) // unit
    source = iota((shards, span), 0)
    first = shards * rows - jnp.sum(jnp.where(source >= lane, wide, 0), axis=0, keepdims=True)
    last = shards * rows - jnp.sum(jnp.where(source > lane, wide, 0), axis=0, keepdims=True)
    inner = lax.rem(index, unit)
    same = inner == lax.rem(iota((1, span), 1), unit)
    for h in range(CHUNKS):
        part = recv_one.at[h, pl.ds(0, len(peers))]
        pltpu.make_async_copy(part, part, one_sem.at[1, h]).wait()
        goal = index // unit * rows + me * tile + unit * h + inner
        mix = (same & (first <= goal) & (goal < last)).astype(jnp.float32).astype(jnp.bfloat16)
        got = pieces(recv_one[h].reshape(span, width))
        send_two[h] = select(mix, got).reshape(shards, unit, width)
        for peer in peers:
            pltpu.make_async_remote_copy(
                send_two.at[h, peer], recv_two.at[h, me], two_sem.at[0, h], two_sem.at[1, h],
                device_id={"shard": peer}, device_id_type=MESH,
            ).start()
        recv_two[h, me] = send_two[h, me]
    for h in range(CHUNKS):
        part = recv_two.at[h, pl.ds(0, len(peers))]
        pltpu.make_async_copy(part, part, two_sem.at[1, h]).wait()
    packed = jnp.concatenate([recv_two[h] for h in range(CHUNKS)], axis=1).reshape(rows, width)
    packed_ref[...] = packed

    filled = jnp.clip((me + 1) * rows - start, 0, rows)
    row_live = iota((rows, width), 0) >= rows - filled
    scale = jnp.maximum(filled.astype(jnp.float32), 1.0)
    mean = jnp.sum(packed, axis=0, keepdims=True) / scale
    spread = jnp.where(row_live, (packed - mean) * (packed - mean), 0.0)
    variance = jnp.sum(spread, axis=0, keepdims=True) / scale
    low = jnp.min(jnp.where(row_live, packed, jnp.inf), axis=0, keepdims=True)
    high = jnp.max(jnp.where(row_live, packed, -jnp.inf), axis=0, keepdims=True)
    low = jnp.where(filled > 0, low, 0.0)
    high = jnp.where(filled > 0, high, 0.0)
    stats_ref[...] = jnp.concatenate([mean, variance, low, high], axis=0)

    for h in range(CHUNKS):
        part = recv_one.at[h, pl.ds(0, len(peers))]
        pltpu.make_async_copy(part, part, one_sem.at[0, h]).wait()
        pltpu.make_async_copy(part, part, two_sem.at[0, h]).wait()
    pltpu.make_async_copy(most, most, kept_sem.at[0]).wait()
    pltpu.make_async_copy(three, three, mask_sem.at[0]).wait()


def on_device(shards, groups, values, keep_mask, row_counts):
    rows, width = values.shape
    unit = rows // shards // CHUNKS
    blocks = pltpu.VMEM((CHUNKS, shards, unit, width), jnp.float32)
    packed, stats = pl.pallas_call(
        kernel,
        out_shape=(
            jax.ShapeDtypeStruct((rows, width), jnp.float32),
            jax.ShapeDtypeStruct((4, width), jnp.float32),
        ),
        in_specs=[pl.BlockSpec(memory_space=pl.ANY)] * 3,
        out_specs=(pl.BlockSpec(memory_space=pltpu.VMEM),) * 2,
        scratch_shapes=[
            pltpu.VMEM((rows, width), jnp.float32),
            pltpu.VMEM((1, width), jnp.int32),
            pltpu.VMEM((groups, 1, width), jnp.int32),
            pltpu.SMEM((1,), jnp.int32),
            pltpu.VMEM((1, width), jnp.int32),
            pltpu.VMEM((shards, 1, width), jnp.int32),
            blocks,
            blocks,
            blocks,
            blocks,
            pltpu.SemaphoreType.DMA((3,)),
            pltpu.SemaphoreType.DMA((2,)),
            pltpu.SemaphoreType.DMA((2,)),
            pltpu.SemaphoreType.DMA((2, CHUNKS)),
            pltpu.SemaphoreType.DMA((2, CHUNKS)),
        ],
        name="compact",
        compiler_params=pltpu.CompilerParams(collective_id=0, has_side_effects=True),
    )(values, keep_mask.reshape(1, width), row_counts)
    return packed, stats[:, None, :]


def solution(mesh):
    in_specs = (P("shard", "col"), P(("shard", "col")), P("shard"))
    out_specs = (P("shard", "col"), P(None, "shard", "col"))
    body = functools.partial(on_device, mesh.shape["shard"], mesh.shape["col"])
    return jax.shard_map(body, mesh=mesh, in_specs=in_specs, out_specs=out_specs, check_vma=False)
```

time: 159 us -> 42.1 us (0.26); the launches traced: 157 us -> 42 us
  other arithmetic: 87.1 us -> 0 us
  Pallas kernels: 0 us -> 38.4 us
  starting transfers between devices: 33.7 us -> 0 us
  waiting for transfers between devices: 22.5 us -> 0 us
  local copies, waits for them, and re-layouts: 8.9 us -> 2.25 us
  matrix products: 2.77 us -> 0 us
    gather x61 -> x0, other arithmetic: 81.9 us -> none  [the longest x59 41.9 us: on_device(): first[local // tile][None, :] <= target[:, None]]
    pallas_call x0 -> x1, Pallas kernels: none -> 38.4 us  [on_device(): pl.pallas_call(kernel, out_shape=(jax.ShapeDtypeStruct((rows, width), jnp...]
    all_to_all x4 -> x0, starting transfers between devices: 33.7 us -> none  [the longest x2 18.6 us: gather_directly(): return lax.all_to_all(copies, axis, split_axis=0, concat_axis=0, tiled=True)]
    all_to_all x4 -> x0, waiting for transfers between devices: 22.5 us -> none  [the longest x1 12.4 us: on_device(): lax.all_to_all(mixed.reshape(shards, tile, width), 'shard', 0, 0)]
    gather x7 -> x0, local copies, waits for them, and re-layouts: 4.71 us -> none  [the longest x4 2.58 us: on_device(): last[local // tile][None, :]]
    dot_general x2 -> x0, matrix products: 2.77 us -> none  [the longest x1 1.45 us: on_device(): jnp.dot(mix, tiles.reshape(rows, width), precision=lax.Precision.HIGHEST)]
    broadcast_in_dim x2 -> x0, local copies, waits for them, and re-layouts: 2.55 us -> none  [gather_directly(): copies = jnp.broadcast_to(value, (lax.axis_size(axis), *value.shape))]
    all_to_all x1 -> x0, other arithmetic: 1.77 us -> none  [gather_directly(): return lax.all_to_all(copies, axis, split_axis=0, concat_axis=0, tiled=True)]
  transfers between devices with their start and end apart: 4 -> 0, of which waited for: 3 -> 0; matrix products, arithmetic and copies ran while one was open for 52% -> 0% of each run, Pallas kernels for 0% -> 0%
where the time goes in v2:
time: 42.1 us; the launch traced here: 42 us
  Pallas kernels  38.4 us (91%)
  local copies, waits for them, and re-layouts  2.25 us (5%)
  between operations  1.29 us (3%)
    pallas_call x1, Pallas kernels, on_device(): pl.pallas_call(kernel, out_shape=(jax.ShapeDtypeStruct((rows, width), jnp...  38.4 us
    unnamed x4, local copies, waits for them, and re-layouts  2.25 us

profile of v2, /device:TPU:1, one launch (start us, length us, event | category | flops | bytes accessed | tf_op | source)
XLA Modules:
  0.0 42.0 jit_solution(11841383640788750332)
XLA Ops:
  1.3 38.4 %compact.1 = (f32[512,128]{1,0:T(8,128)}, f32[4,128]{1,0:T(4,128)}) custom-call(f32[512,128]{1,0:T(8,128)} %values_ref.1, s32[1,128]{1,0:T(1,128)} %bitcast.5, s32[1]{0:T(128)S(6)} %copy.8.counts_ref), custom_call_target="tpu_custom_call" | custom-call | tf_op jit(solution)/shard_map/compact/pallas_call | solution.py:202
  39.7 0.0 copy-start
  39.7 1.7 %copy.9 = f32[512,128]{1,0:T(8,128)} copy(f32[512,128]{1,0:T(8,128)} %get-tuple-element.10) | data formatting | bytes 524288
  41.4 0.0 copy-done
  41.4 0.6 %copy.10 = f32[4,1,128]{2,1,0:T(1,128)} copy(f32[4,1,128]{2,1,0:T(1,128)S(1)} %bitcast.4) | data formatting | bytes 4096
Async XLA Ops:
  39.7 1.7 %copy-start = (f32[4,128]{1,0:T(4,128)S(1)}, f32[4,128]{1,0:T(4,128)}, u32[]{:S(2)}) copy-start(f32[4,128]{1,0:T(4,128)} %get-tuple-element.5) | copy-start | bytes 6148

commit v3 on v2

--- a/solution.py
+++ b/solution.py
@@ -8,7 +8,7 @@
 from jax.sharding import PartitionSpec as P
 
 MESH = pl.DeviceIdType.MESH
-CHUNKS = 2
+CHUNKS = 4
 SIZES = (8, 4, 2)
 
 
@@ -19,6 +19,12 @@
 STEPS = sorted(
     [(z, y, c) for z in range(8) for y in range(4) for c in range(2)][1:],
     key=lambda step: (-hops(step), step),
+)
+
+
+PLANE = sorted(
+    [(y, c, x) for y in range(4) for c in range(2) for x in range(4)][1:],
+    key=lambda step: (-min(step[0], 4 - step[0]) - min(step[2], 4 - step[2]), step),
 )
 
 
@@ -51,19 +57,24 @@
     mask_buf,
     counts_buf,
     kept_own,
-    kept_buf,
+    line_buf,
+    line_own,
+    plane_buf,
     send_one,
     recv_one,
     send_two,
     recv_two,
     local_sem,
     mask_sem,
-    kept_sem,
+    line_sem,
+    plane_sem,
     one_sem,
     two_sem,
 ):
     rows, width = values_buf.shape
-    shards = kept_buf.shape[0]
+    shards = send_one.shape[1]
+    groups = mask_buf.shape[0]
+    depth, breadth = SIZES[0], SIZES[1] * SIZES[2]
     unit = send_one.shape[2]
     span = shards * unit
     tile = rows // shards
@@ -83,52 +94,82 @@
         for dz, dy, dc in STEPS
     ]
     cols = [lax.rem(col + d, 4) for d in (2, 1, 3)]
+    lines = [lax.rem(z + dz, 8) * 8 + lax.rem(me, 8) for dz in (4, 3, 5, 2, 6, 1, 7)]
+    planes = [
+        {"shard": z * 8 + lax.rem(y + dy, 4) * 2 + lax.rem(c + dc, 2), "col": lax.rem(col + dx, 4)}
+        for dy, dc, dx in PLANE
+    ]
 
     barrier = pltpu.get_barrier_semaphore()
-    for peer in peers:
+    for peer in lines:
         pl.semaphore_signal(barrier, inc=1, device_id={"shard": peer}, device_id_type=MESH)
-    for peer in cols:
-        pl.semaphore_signal(barrier, inc=1, device_id={"col": peer}, device_id_type=MESH)
+    for peer in planes:
+        pl.semaphore_signal(barrier, inc=1, device_id=peer, device_id_type=MESH)
     load_mask.wait()
     load_counts.wait()
-    pl.semaphore_wait(barrier, len(peers) + len(cols))
-
+    present = counts_buf[0]
+    mine = (mask_own[...] == 1) & (col * width + iota((1, width), 1) < present)
+    kept = jnp.sum(jnp.where(mine, 1, 0), axis=1, keepdims=True)
+    kept_own[...] = jnp.broadcast_to(kept, (1, width))
+    pl.semaphore_wait(barrier, len(lines) + len(planes))
+
+    for peer in lines:
+        pltpu.make_async_remote_copy(
+            kept_own, line_buf.at[z], line_sem.at[0], line_sem.at[1],
+            device_id={"shard": peer}, device_id_type=MESH,
+        ).start()
     for peer in cols:
         pltpu.make_async_remote_copy(
             mask_own, mask_buf.at[col], mask_sem.at[0], mask_sem.at[1],
             device_id={"col": peer}, device_id_type=MESH,
         ).start()
+    line_buf[z] = kept_own[...]
     mask_buf[col] = mask_own[...]
+    line_part = line_buf.at[pl.ds(0, len(lines))]
+    pltpu.make_async_copy(line_part, line_part, line_sem.at[1]).wait()
+    level = iota((1, width), 1) // (width // depth)
+    line = line_buf[0]
+    for k in range(1, depth):
+        line = jnp.where(level == k, line_buf[k], line)
+    line_own[...] = line
+    place_in_plane = lax.rem(me, breadth) * groups + col
+    for peer in planes:
+        pltpu.make_async_remote_copy(
+            line_own, plane_buf.at[place_in_plane], plane_sem.at[0], plane_sem.at[1],
+            device_id=peer, device_id_type=MESH,
+        ).start()
+    plane_buf[place_in_plane] = line_own[...]
+
     load_values.wait()
     parts = pieces(values_buf[...])
     three = mask_buf.at[pl.ds(0, len(cols))]
     pltpu.make_async_copy(three, three, mask_sem.at[1]).wait()
-
-    groups = mask_buf.shape[0]
     mask = jnp.concatenate([mask_buf[g] for g in range(groups)], axis=0)
     row = iota((groups, width), 0) * width + iota((groups, width), 1)
-    live = (mask == 1) & (row < counts_buf[0])
+    live = (mask == 1) & (row < present)
     live_part = jnp.where(live, 1.0, 0.0).astype(jnp.bfloat16)
     ahead = (iota((width, width), 0) < iota((width, width), 1)).astype(jnp.float32).astype(jnp.bfloat16)
     inside = jnp.dot(live_part, ahead, preferred_element_type=jnp.float32)
     ones = jnp.ones((width, width), jnp.bfloat16)
     whole = jnp.dot(live_part, ones, preferred_element_type=jnp.float32)
-    kept = jnp.sum(whole, axis=0, keepdims=True)
-    kept_own[...] = kept.astype(jnp.int32)
-    for peer in peers:
-        pltpu.make_async_remote_copy(
-            kept_own, kept_buf.at[me], kept_sem.at[0], kept_sem.at[1],
-            device_id={"shard": peer}, device_id_type=MESH,
-        ).start()
-    kept_buf[me] = kept_own[...]
     base = [jnp.zeros((1, width), jnp.float32)]
     for g in range(groups - 1):
         base.append(base[-1] + whole[g : g + 1])
     rank = (inside + jnp.concatenate(base, axis=0)).astype(jnp.int32)
-    most = kept_buf.at[pl.ds(0, len(peers))]
-    pltpu.make_async_copy(most, most, kept_sem.at[1]).wait()
-
-    every = jnp.concatenate([kept_buf[i] for i in range(shards)], axis=0)
+    plane_part = plane_buf.at[pl.ds(0, len(planes))]
+    pltpu.make_async_copy(plane_part, plane_part, plane_sem.at[1]).wait()
+
+    plane = [
+        sum(plane_buf[b * groups + g] for g in range(1, groups)) + plane_buf[b * groups] for b in range(breadth)
+    ]
+    plane = jnp.concatenate(plane, axis=0)
+    every = jnp.concatenate(
+        [
+            jnp.broadcast_to(plane[:, k * (width // depth) : k * (width // depth) + 1], (breadth, width))
+            for k in range(depth)
+        ],
+        axis=0,
+    )
     shard = iota((shards, width), 0)
     mine = shards * rows - jnp.sum(jnp.where(shard >= me, every, 0), axis=0, keepdims=True)
     start = shards * rows - jnp.sum(every, axis=0, keepdims=True)
@@ -185,14 +226,25 @@
     high = jnp.max(jnp.where(row_live, packed, -jnp.inf), axis=0, keepdims=True)
     low = jnp.where(filled > 0, low, 0.0)
     high = jnp.where(filled > 0, high, 0.0)
-    stats_ref[...] = jnp.concatenate([mean, variance, low, high], axis=0)
+    for place, stat in enumerate((mean, variance, low, high)):
+        stats_ref[place] = stat
 
     for h in range(CHUNKS):
         part = recv_one.at[h, pl.ds(0, len(peers))]
         pltpu.make_async_copy(part, part, one_sem.at[0, h]).wait()
         pltpu.make_async_copy(part, part, two_sem.at[0, h]).wait()
-    pltpu.make_async_copy(most, most, kept_sem.at[0]).wait()
+    pltpu.make_async_copy(line_part, line_part, line_sem.at[0]).wait()
+    pltpu.make_async_copy(plane_part, plane_part, plane_sem.at[0]).wait()
     pltpu.make_async_copy(three, three, mask_sem.at[0]).wait()
+
+
+def deliver(packed_ref, stats_ref, packed_out, stats_out, sem):
+    rows = pltpu.make_async_copy(packed_ref, packed_out, sem.at[0])
+    stats = pltpu.make_async_copy(stats_ref, stats_out, sem.at[1])
+    rows.start()
+    stats.start()
+    rows.wait()
+    stats.wait()
 
 
 def on_device(shards, groups, values, keep_mask, row_counts):
@@ -203,9 +255,9 @@
         kernel,
         out_shape=(
             jax.ShapeDtypeStruct((rows, width), jnp.float32),
-            jax.ShapeDtypeStruct((4, width), jnp.float32),
+            jax.ShapeDtypeStruct((4, 1, width), jnp.float32),
         ),
-        in_specs=[pl.BlockSpec(memory_space=pl.ANY)] * 3,
+        in_specs=[pl.BlockSpec(memory_space=pltpu.HBM)] * 3,
         out_specs=(pl.BlockSpec(memory_space=pltpu.VMEM),) * 2,
         scratch_shapes=[
             pltpu.VMEM((rows, width), jnp.float32),
@@ -213,7 +265,9 @@
             pltpu.VMEM((groups, 1, width), jnp.int32),
             pltpu.SMEM((1,), jnp.int32),
             pltpu.VMEM((1, width), jnp.int32),
-            pltpu.VMEM((shards, 1, width), jnp.int32),
+            pltpu.VMEM((SIZES[0], 1, width), jnp.int32),
+            pltpu.VMEM((1, width), jnp.int32),
+            pltpu.VMEM((SIZES[1] * SIZES[2] * groups, 1, width), jnp.int32),
             blocks,
             blocks,
             blocks,
@@ -221,13 +275,30 @@
             pltpu.SemaphoreType.DMA((3,)),
             pltpu.SemaphoreType.DMA((2,)),
             pltpu.SemaphoreType.DMA((2,)),
+            pltpu.SemaphoreType.DMA((2,)),
             pltpu.SemaphoreType.DMA((2, CHUNKS)),
             pltpu.SemaphoreType.DMA((2, CHUNKS)),
         ],
         name="compact",
-        compiler_params=pltpu.CompilerParams(collective_id=0, has_side_effects=True),
-    )(values, keep_mask.reshape(1, width), row_counts)
-    return packed, stats[:, None, :]
+        compiler_params=pltpu.CompilerParams(collective_id=0, has_side_effects=True, vmem_limit_bytes=8 * 1024 * 1024),
+    )(
+        pltpu.with_memory_space_constraint(values, pltpu.HBM),
+        pltpu.with_memory_space_constraint(keep_mask.reshape(1, width), pltpu.HBM),
+        row_counts,
+    )
+    whole = pl.BlockSpec(memory_space=pltpu.VMEM)
+    return pl.pallas_call(
+        deliver,
+        out_shape=(
+            jax.ShapeDtypeStruct((rows, width), jnp.float32),
+            jax.ShapeDtypeStruct((4, 1, width), jnp.float32),
+        ),
+        in_specs=[pl.BlockSpec(memory_space=pl.ANY)] * 2,
+        out_specs=(pl.BlockSpec(memory_space=pltpu.HBM),) * 2,
+        scratch_shapes=[pltpu.SemaphoreType.DMA((2,))],
+        name="deliver",
+        compiler_params=pltpu.CompilerParams(vmem_limit_bytes=1024 * 1024),
+    )(packed, stats)
 
 
 def solution(mesh):

time: 42.1 us -> 38.8 us (0.922)
  local copies, waits for them, and re-layouts: 2.25 us -> 0 us
  Pallas kernels: 38.4 us -> 37.4 us
    unnamed x4 -> x0, local copies, waits for them, and re-layouts: 2.25 us -> none
    pallas_call x1, Pallas kernels: 38.4 us -> 36.7 us  [on_device(): pl.pallas_call(kernel, out_shape=(jax.ShapeDtypeStruct((rows, width), jnp...]
    pallas_call x0 -> x1, Pallas kernels: none -> 0.72 us  [on_device(): pl.pallas_call(deliver, out_shape=(jax.ShapeDtypeStruct((rows, width), jn...]
where the time goes in v3:
time: 38.8 us; the launch traced here: 38.7 us
  Pallas kernels  37.4 us (96%)
  between operations  1.28 us (3%)
    pallas_call x1, Pallas kernels, on_device(): pl.pallas_call(kernel, out_shape=(jax.ShapeDtypeStruct((rows, width), jnp...  36.7 us

profile of v3, /device:TPU:1, one launch (start us, length us, event | category | flops | bytes accessed | tf_op | source)
XLA Modules:
  0.0 38.7 jit_solution(14966791232477266721)
XLA Ops:
  1.3 36.7 %compact.1 = (f32[512,128]{1,0:T(8,128)S(1)}, f32[4,1,128]{2,1,0:T(1,128)S(1)}) custom-call(f32[512,128]{1,0:T(8,128)} %values_ref.1, s32[1,128]{1,0:T(1,128)} %bitcast.1, s32[1]{0:T(128)S(6)} %copy.5.counts_ref), custom_call_target="tpu_custom_call" | custom-call | tf_op jit(solution)/shard_map/compact/pallas_call | solution.py:254
  38.0 0.7 %deliver.1 = (f32[512,128]{1,0:T(8,128)}, f32[4,1,128]{2,1,0:T(1,128)}) custom-call(f32[512,128]{1,0:T(8,128)S(1)} %get-tuple-element.4.packed_ref, f32[4,1,128]{2,1,0:T(1,128)S(1)} %get-tuple-element.5.stats_ref), custom_call_target="tpu_custom_call" | custom-call | tf_op jit(solution)/shard_map/deliver/pallas_call | solution.py:290

commit v4 on v3

--- a/solution.py
+++ b/solution.py
@@ -18,7 +18,7 @@
 
 STEPS = sorted(
     [(z, y, c) for z in range(8) for y in range(4) for c in range(2)][1:],
-    key=lambda step: (-hops(step), step),
+    key=lambda step: (-hops(step), -min(step[0], 8 - step[0]), step),
 )
 
 
@@ -51,7 +51,7 @@
     mask_ref,
     counts_ref,
     packed_ref,
-    stats_ref,
+    filled_ref,
     values_buf,
     mask_own,
     mask_buf,
@@ -63,7 +63,6 @@
     send_one,
     recv_one,
     send_two,
-    recv_two,
     local_sem,
     mask_sem,
     line_sem,
@@ -206,29 +205,14 @@
         send_two[h] = select(mix, got).reshape(shards, unit, width)
         for peer in peers:
             pltpu.make_async_remote_copy(
-                send_two.at[h, peer], recv_two.at[h, me], two_sem.at[0, h], two_sem.at[1, h],
+                send_two.at[h, peer], packed_ref.at[me, pl.ds(unit * h, unit)], two_sem.at[0, h], two_sem.at[1, h],
                 device_id={"shard": peer}, device_id_type=MESH,
             ).start()
-        recv_two[h, me] = send_two[h, me]
+        packed_ref[me, unit * h : unit * (h + 1)] = send_two[h, me]
+    filled_ref[...] = jnp.clip((me + 1) * rows - start, 0, rows)
     for h in range(CHUNKS):
-        part = recv_two.at[h, pl.ds(0, len(peers))]
+        part = packed_ref.at[pl.ds(0, len(peers)), pl.ds(unit * h, unit)]
         pltpu.make_async_copy(part, part, two_sem.at[1, h]).wait()
-    packed = jnp.concatenate([recv_two[h] for h in range(CHUNKS)], axis=1).reshape(rows, width)
-    packed_ref[...] = packed
-
-    filled = jnp.clip((me + 1) * rows - start, 0, rows)
-    row_live = iota((rows, width), 0) >= rows - filled
-    scale = jnp.maximum(filled.astype(jnp.float32), 1.0)
-    mean = jnp.sum(packed, axis=0, keepdims=True) / scale
-    spread = jnp.where(row_live, (packed - mean) * (packed - mean), 0.0)
-    variance = jnp.sum(spread, axis=0, keepdims=True) / scale
-    low = jnp.min(jnp.where(row_live, packed, jnp.inf), axis=0, keepdims=True)
-    high = jnp.max(jnp.where(row_live, packed, -jnp.inf), axis=0, keepdims=True)
-    low = jnp.where(filled > 0, low, 0.0)
-    high = jnp.where(filled > 0, high, 0.0)
-    for place, stat in enumerate((mean, variance, low, high)):
-        stats_ref[place] = stat
-
     for h in range(CHUNKS):
         part = recv_one.at[h, pl.ds(0, len(peers))]
         pltpu.make_async_copy(part, part, one_sem.at[0, h]).wait()
@@ -238,12 +222,30 @@
     pltpu.make_async_copy(three, three, mask_sem.at[0]).wait()
 
 
-def deliver(packed_ref, stats_ref, packed_out, stats_out, sem):
-    rows = pltpu.make_async_copy(packed_ref, packed_out, sem.at[0])
-    stats = pltpu.make_async_copy(stats_ref, stats_out, sem.at[1])
-    rows.start()
+def deliver(packed_ref, filled_ref, packed_out, stats_out, stats_buf, sem):
+    shards, tile, width = packed_ref.shape
+    rows = shards * tile
+    leave = pltpu.make_async_copy(packed_ref, packed_out, sem.at[0])
+    leave.start()
+    filled = filled_ref[...]
+    scale = jnp.maximum(filled.astype(jnp.float32), 1.0)
+    slot = iota((shards, tile, width), 0) * tile + iota((shards, tile, width), 1)
+    row_live = slot >= (rows - filled)[:, None]
+    packed = packed_ref[...]
+    total = jnp.sum(jnp.sum(packed, axis=0), axis=0, keepdims=True)
+    low = jnp.min(jnp.min(jnp.where(row_live, packed, jnp.inf), axis=0), axis=0, keepdims=True)
+    high = jnp.max(jnp.max(jnp.where(row_live, packed, -jnp.inf), axis=0), axis=0, keepdims=True)
+    mean = total / scale
+    away = packed - mean[None]
+    spread = jnp.where(row_live, away * away, 0.0)
+    variance = jnp.sum(jnp.sum(spread, axis=0), axis=0, keepdims=True) / scale
+    low = jnp.where(filled > 0, low, 0.0)
+    high = jnp.where(filled > 0, high, 0.0)
+    for place, stat in enumerate((mean, variance, low, high)):
+        stats_buf[place] = stat
+    stats = pltpu.make_async_copy(stats_buf, stats_out, sem.at[1])
     stats.start()
-    rows.wait()
+    leave.wait()
     stats.wait()
 
 
@@ -251,11 +253,11 @@
     rows, width = values.shape
     unit = rows // shards // CHUNKS
     blocks = pltpu.VMEM((CHUNKS, shards, unit, width), jnp.float32)
-    packed, stats = pl.pallas_call(
+    packed, filled = pl.pallas_call(
         kernel,
         out_shape=(
-            jax.ShapeDtypeStruct((rows, width), jnp.float32),
-            jax.ShapeDtypeStruct((4, 1, width), jnp.float32),
+            jax.ShapeDtypeStruct((shards, rows // shards, width), jnp.float32),
+            jax.ShapeDtypeStruct((1, width), jnp.int32),
         ),
         in_specs=[pl.BlockSpec(memory_space=pltpu.HBM)] * 3,
         out_specs=(pl.BlockSpec(memory_space=pltpu.VMEM),) * 2,
@@ -268,7 +270,6 @@
             pltpu.VMEM((SIZES[0], 1, width), jnp.int32),
             pltpu.VMEM((1, width), jnp.int32),
             pltpu.VMEM((SIZES[1] * SIZES[2] * groups, 1, width), jnp.int32),
-            blocks,
             blocks,
             blocks,
             blocks,
@@ -286,19 +287,19 @@
         pltpu.with_memory_space_constraint(keep_mask.reshape(1, width), pltpu.HBM),
         row_counts,
     )
-    whole = pl.BlockSpec(memory_space=pltpu.VMEM)
-    return pl.pallas_call(
+    packed, stats = pl.pallas_call(
         deliver,
         out_shape=(
-            jax.ShapeDtypeStruct((rows, width), jnp.float32),
+            jax.ShapeDtypeStruct((shards, rows // shards, width), jnp.float32),
             jax.ShapeDtypeStruct((4, 1, width), jnp.float32),
         ),
-        in_specs=[pl.BlockSpec(memory_space=pl.ANY)] * 2,
+        in_specs=[pl.BlockSpec(memory_space=pltpu.VMEM)] * 2,
         out_specs=(pl.BlockSpec(memory_space=pltpu.HBM),) * 2,
-        scratch_shapes=[pltpu.SemaphoreType.DMA((2,))],
+        scratch_shapes=[pltpu.VMEM((4, 1, width), jnp.float32), pltpu.SemaphoreType.DMA((2,))],
         name="deliver",
         compiler_params=pltpu.CompilerParams(vmem_limit_bytes=1024 * 1024),
-    )(packed, stats)
+    )(packed, filled)
+    return packed.reshape(rows, width), stats
 
 
 def solution(mesh):

time: 38.8 us -> 38.4 us (0.990)
  no operation moved by 1% of the time
where the time goes in v4:
time: 38.4 us; the launch traced here: 38.3 us
  Pallas kernels  37.1 us (97%)
  between operations  1.28 us (3%)
    pallas_call x1, Pallas kernels, on_device(): pl.pallas_call(kernel, out_shape=(jax.ShapeDtypeStruct((shards, rows // s...  36.2 us
    pallas_call x1, Pallas kernels, on_device(): pl.pallas_call(deliver, out_shape=(jax.ShapeDtypeStruct((shards, rows //...  0.82 us

profile of v4, /device:TPU:1, one launch (start us, length us, event | category | flops | bytes accessed | tf_op | source)
XLA Modules:
  0.0 38.3 jit_solution(7497290598484452314)
XLA Ops:
  1.3 36.2 %compact.1 = (f32[64,8,128]{2,1,0:T(8,128)S(1)}, s32[1,128]{1,0:T(1,128)S(1)}) custom-call(f32[512,128]{1,0:T(8,128)} %values_ref.1, s32[1,128]{1,0:T(1,128)} %bitcast.2, s32[1]{0:T(128)S(6)} %copy.5.counts_ref), custom_call_target="tpu_custom_call" | custom-call | tf_op jit(solution)/shard_map/compact/pallas_call | solution.py:256
  37.5 0.8 %deliver.1 = (f32[64,8,128]{2,1,0:T(8,128)}, f32[4,1,128]{2,1,0:T(1,128)}) custom-call(f32[64,8,128]{2,1,0:T(8,128)S(1)} %get-tuple-element.6.packed_ref, s32[1,128]{1,0:T(1,128)S(1)} %get-tuple-element.7.filled_ref), custom_call_target="tpu_custom_call" | custom-call | tf_op jit(solution)/shard_map/deliver/pallas_call | solution.py:290

commit v5 on v4

--- a/solution.py
+++ b/solution.py
@@ -18,7 +18,7 @@
 
 STEPS = sorted(
     [(z, y, c) for z in range(8) for y in range(4) for c in range(2)][1:],
-    key=lambda step: (-hops(step), -min(step[0], 8 - step[0]), step),
+    key=lambda step: (-hops(step), (step[0] * 5 + step[1] * 3 + step[2] * 7) % 11, step),
 )
 
 
@@ -99,6 +99,15 @@
         for dy, dc, dx in PLANE
     ]
 
+    near = [z * 8 + lax.rem(y + dy, 4) * 2 + lax.rem(c + dc, 2) for dy, dc in ((2, 1), (2, 0), (1, 1), (3, 1), (1, 0), (3, 0), (0, 1))]
+    climb = [
+        (step - 1 + (step + 7 - z) // 8) * 8 + lax.rem(y + dy, 4) * 2 + lax.rem(c + dc, 2)
+        for step in range(1, 8)
+        for dy in (2, 1, 3, 0)
+        for dc in (1, 0)
+    ]
+    early, late = near + climb[: 32], climb[32 :]
+
     barrier = pltpu.get_barrier_semaphore()
     for peer in lines:
         pl.semaphore_signal(barrier, inc=1, device_id={"shard": peer}, device_id_type=MESH)
@@ -203,12 +212,18 @@
         mix = (same & (first <= goal) & (goal < last)).astype(jnp.float32).astype(jnp.bfloat16)
         got = pieces(recv_one[h].reshape(span, width))
         send_two[h] = select(mix, got).reshape(shards, unit, width)
-        for peer in peers:
+        for peer in early:
             pltpu.make_async_remote_copy(
                 send_two.at[h, peer], packed_ref.at[me, pl.ds(unit * h, unit)], two_sem.at[0, h], two_sem.at[1, h],
                 device_id={"shard": peer}, device_id_type=MESH,
             ).start()
         packed_ref[me, unit * h : unit * (h + 1)] = send_two[h, me]
+    for h in range(CHUNKS):
+        for peer in late:
+            pltpu.make_async_remote_copy(
+                send_two.at[h, peer], packed_ref.at[me, pl.ds(unit * h, unit)], two_sem.at[0, h], two_sem.at[1, h],
+                device_id={"shard": peer}, device_id_type=MESH,
+            ).start()
     filled_ref[...] = jnp.clip((me + 1) * rows - start, 0, rows)
     for h in range(CHUNKS):
         part = packed_ref.at[pl.ds(0, len(peers)), pl.ds(unit * h, unit)]

time: 38.4 us -> 37.9 us (0.987)
  Pallas kernels: 37.1 us -> 36.5 us
    pallas_call x1, Pallas kernels: 36.2 us -> 35.6 us  [on_device(): pl.pallas_call(kernel, out_shape=(jax.ShapeDtypeStruct((shards, rows // s...]
where the time goes in v5:
time: 37.9 us; the launch traced here: 37.7 us
  Pallas kernels  36.5 us (96%)
  between operations  1.28 us (3%)
    pallas_call x1, Pallas kernels, on_device(): pl.pallas_call(kernel, out_shape=(jax.ShapeDtypeStruct((shards, rows // s...  35.6 us
    pallas_call x1, Pallas kernels, on_device(): pl.pallas_call(deliver, out_shape=(jax.ShapeDtypeStruct((shards, rows //...  0.82 us

profile of v5, /device:TPU:1, one launch (start us, length us, event | category | flops | bytes accessed | tf_op | source)
XLA Modules:
  0.0 37.7 jit_solution(14175905330744009431)
XLA Ops:
  1.3 35.6 %compact.1 = (f32[64,8,128]{2,1,0:T(8,128)S(1)}, s32[1,128]{1,0:T(1,128)S(1)}) custom-call(f32[512,128]{1,0:T(8,128)} %values_ref.1, s32[1,128]{1,0:T(1,128)} %bitcast.2, s32[1]{0:T(128)S(6)} %copy.5.counts_ref), custom_call_target="tpu_custom_call" | custom-call | tf_op jit(solution)/shard_map/compact/pallas_call | solution.py:271
  36.9 0.8 %deliver.1 = (f32[64,8,128]{2,1,0:T(8,128)}, f32[4,1,128]{2,1,0:T(1,128)}) custom-call(f32[64,8,128]{2,1,0:T(8,128)S(1)} %get-tuple-element.6.packed_ref, s32[1,128]{1,0:T(1,128)S(1)} %get-tuple-element.7.filled_ref), custom_call_target="tpu_custom_call" | custom-call | tf_op jit(solution)/shard_map/deliver/pallas_call | solution.py:305

commit v6 on v5

--- a/solution.py
+++ b/solution.py
@@ -88,25 +88,12 @@
     load_values.start()
 
     z, y, c = me // 8, lax.rem(me // 2, 4), lax.rem(me, 2)
-    peers = [
-        lax.rem(z + dz, 8) * 8 + lax.rem(y + dy, 4) * 2 + lax.rem(c + dc, 2)
-        for dz, dy, dc in STEPS
-    ]
     cols = [lax.rem(col + d, 4) for d in (2, 1, 3)]
     lines = [lax.rem(z + dz, 8) * 8 + lax.rem(me, 8) for dz in (4, 3, 5, 2, 6, 1, 7)]
     planes = [
         {"shard": z * 8 + lax.rem(y + dy, 4) * 2 + lax.rem(c + dc, 2), "col": lax.rem(col + dx, 4)}
         for dy, dc, dx in PLANE
     ]
-
-    near = [z * 8 + lax.rem(y + dy, 4) * 2 + lax.rem(c + dc, 2) for dy, dc in ((2, 1), (2, 0), (1, 1), (3, 1), (1, 0), (3, 0), (0, 1))]
-    climb = [
-        (step - 1 + (step + 7 - z) // 8) * 8 + lax.rem(y + dy, 4) * 2 + lax.rem(c + dc, 2)
-        for step in range(1, 8)
-        for dy in (2, 1, 3, 0)
-        for dc in (1, 0)
-    ]
-    early, late = near + climb[: 32], climb[32 :]
 
     barrier = pltpu.get_barrier_semaphore()
     for peer in lines:
@@ -125,11 +112,6 @@
         pltpu.make_async_remote_copy(
             kept_own, line_buf.at[z], line_sem.at[0], line_sem.at[1],
             device_id={"shard": peer}, device_id_type=MESH,
-        ).start()
-    for peer in cols:
-        pltpu.make_async_remote_copy(
-            mask_own, mask_buf.at[col], mask_sem.at[0], mask_sem.at[1],
-            device_id={"col": peer}, device_id_type=MESH,
         ).start()
     line_buf[z] = kept_own[...]
     mask_buf[col] = mask_own[...]
@@ -146,7 +128,25 @@
             line_own, plane_buf.at[place_in_plane], plane_sem.at[0], plane_sem.at[1],
             device_id=peer, device_id_type=MESH,
         ).start()
+    for peer in cols:
+        pltpu.make_async_remote_copy(
+            mask_own, mask_buf.at[col], mask_sem.at[0], mask_sem.at[1],
+            device_id={"col": peer}, device_id_type=MESH,
+        ).start()
     plane_buf[place_in_plane] = line_own[...]
+
+    peers = [
+        lax.rem(z + dz, 8) * 8 + lax.rem(y + dy, 4) * 2 + lax.rem(c + dc, 2)
+        for dz, dy, dc in STEPS
+    ]
+    near = [z * 8 + lax.rem(y + dy, 4) * 2 + lax.rem(c + dc, 2) for dy, dc in ((2, 1), (2, 0), (1, 1), (3, 1), (1, 0), (3, 0), (0, 1))]
+    climb = [
+        (step - 1 + (step + 7 - z) // 8) * 8 + row * 2 + core
+        for step in range(1, 8)
+        for row in (0, 1, 3, 2)
+        for core in (0, 1)
+    ]
+    early, late = near + climb[: 32], climb[32 :]
 
     load_values.wait()
     parts = pieces(values_buf[...])

time: 37.9 us -> 37.8 us (level)
  no operation moved by 1% of the time
where the time goes in v6:
time: 37.8 us; the launch traced here: 37.7 us
  Pallas kernels  36.5 us (97%)
  between operations  1.28 us (3%)
    pallas_call x1, Pallas kernels, on_device(): pl.pallas_call(kernel, out_shape=(jax.ShapeDtypeStruct((shards, rows // s...  35.6 us
    pallas_call x1, Pallas kernels, on_device(): pl.pallas_call(deliver, out_shape=(jax.ShapeDtypeStruct((shards, rows //...  0.82 us

profile of v6, /device:TPU:1, one launch (start us, length us, event | category | flops | bytes accessed | tf_op | source)
XLA Modules:
  0.0 37.7 jit_solution(14336302564253135218)
XLA Ops:
  1.3 35.6 %compact.1 = (f32[64,8,128]{2,1,0:T(8,128)S(1)}, s32[1,128]{1,0:T(1,128)S(1)}) custom-call(f32[512,128]{1,0:T(8,128)} %values_ref.1, s32[1,128]{1,0:T(1,128)} %bitcast.2, s32[1]{0:T(128)S(6)} %copy.5.counts_ref), custom_call_target="tpu_custom_call" | custom-call | tf_op jit(solution)/shard_map/compact/pallas_call | solution.py:271
  36.9 0.8 %deliver.1 = (f32[64,8,128]{2,1,0:T(8,128)}, f32[4,1,128]{2,1,0:T(1,128)}) custom-call(f32[64,8,128]{2,1,0:T(8,128)S(1)} %get-tuple-element.6.packed_ref, s32[1,128]{1,0:T(1,128)S(1)} %get-tuple-element.7.filled_ref), custom_call_target="tpu_custom_call" | custom-call | tf_op jit(solution)/shard_map/deliver/pallas_call | solution.py:305
